TPU v7x, 512 devices: a whole 4x8x8 slice. The times are simulated.
512 devices in a mesh: rows: 512 (over z, y, x, core).
Axes of the slice: x: 4, y: 8, z: 8, core: 2. Of those that a mesh axis runs over, the one named last changes fastest.
Arguments:
- adj_diag: int32 [8192, 512], P('rows'), may hold values from -2147483648 to 2147483647
- adj_right: int32 [8192, 512], P('rows'), may hold values from -2147483648 to 2147483647
- alive_diag: int32 [8192, 512], P('rows'), may hold values from -2147483648 to 2147483647
- alive_right: int32 [8192, 512], P('rows'), may hold values from -2147483648 to 2147483647
- truss_k: int32 [1], replicated, may hold values from 130 to 193
Outputs:
- support_field: float32 [262144, 1024], P('rows')
- removed_counts: int32 [3], replicated
All inputs are finite; a program needn't handle non-finite values.
Results may differ from a plain program's by a relative error of at most 0.0003.
Values may be sent and summed in bfloat16 or wider, within the bound.
No kernel may reach another device: no remote copies, remote signals or barrier semaphores. Data moves between devices by JAX's collectives and lax.ppermute only.
A program may use at most 64 MiB of HBM per device.

v0:
```python
import jax
import jax.numpy as jnp
from jax import lax
from jax.sharding import Mesh
from jax.sharding import PartitionSpec as P

ITERS = 3
ROWS = ("rows_0", "rows_1", "rows_2", "rows_3")


def shifted(array, axis, by):
    count = lax.axis_size(axis)
    return lax.ppermute(array, axis, [(i, (i + by) % count) for i in range(count)])


def over_axes(array, axes):
    for axis in axes:
        array = lax.psum(array, axis)
    return array


def unpack_tile(packed):
    shifts = jnp.arange(32, dtype=jnp.int32)
    tile_bits = packed[:, None, :] >> shifts[None, :, None] & 1
    return tile_bits.reshape(packed.shape[0] * 32, packed.shape[1])


def pack_bits(tile_bits):
    shifts = jnp.arange(32, dtype=jnp.int32)
    sectioned = tile_bits.reshape(tile_bits.shape[0] // 32, 32, tile_bits.shape[1])
    return jnp.sum(sectioned << shifts[None, :, None], axis=1, dtype=jnp.int32)


def within_tile(packed):
    upper_half = jnp.triu(unpack_tile(packed), 1)
    return (upper_half + upper_half.T).astype(jnp.bfloat16)


def across_tile(packed):
    return unpack_tile(packed).astype(jnp.bfloat16)


def pack_across(across):
    return pack_bits(across.astype(jnp.int32))


def fold_within(within):
    width = within.shape[0]
    half = width // 2
    row_ids = lax.broadcasted_iota(jnp.int32, (half, width), 0)
    col_ids = lax.broadcasted_iota(jnp.int32, (half, width), 1)
    flipped = within[half:][::-1, ::-1]
    folded = jnp.where(col_ids > row_ids, within[:half], flipped)
    return pack_bits(folded.astype(jnp.int32))


def unfold_within(packed):
    folded = unpack_tile(packed)
    half = folded.shape[0]
    width = folded.shape[1]
    row_ids = lax.broadcasted_iota(jnp.int32, (half, width), 0)
    col_ids = lax.broadcasted_iota(jnp.int32, (half, width), 1)
    top_rows = jnp.where(col_ids > row_ids, folded, jnp.zeros_like(folded))
    bottom_rows = jnp.where(col_ids < row_ids, folded, jnp.zeros_like(folded))[::-1, ::-1]
    upper_half = jnp.concatenate([top_rows, bottom_rows], axis=0)
    return (upper_half + upper_half.T).astype(jnp.bfloat16)


def support_within(prev_across, within, across):
    inside = lax.dot_general(
        prev_across, prev_across, (((0,), (0,)), ((), ())), preferred_element_type=jnp.float32
    )
    inside = inside + jnp.dot(within, within, preferred_element_type=jnp.float32)
    return inside + lax.dot_general(
        across, across, (((1,), (1,)), ((), ())), preferred_element_type=jnp.float32
    )


def support_across(within, across, next_within):
    between = jnp.dot(within, across, preferred_element_type=jnp.float32)
    return between + jnp.dot(across, next_within, preferred_element_type=jnp.float32)


def keep_edges(support, tile_mask, thresh):
    return jnp.where(support >= thresh, tile_mask, jnp.zeros_like(tile_mask))


def peel(prev_across, within, across, next_within, thresh):
    inside = support_within(prev_across, within, across)
    between = support_across(within, across, next_within)
    return (
        inside,
        between,
        keep_edges(inside, within, thresh),
        keep_edges(between, across, thresh),
    )


def tally(within, new_within, across, new_across):
    removed = jnp.sum((within - new_within).astype(jnp.int32)) // 2
    removed = removed + jnp.sum((across - new_across).astype(jnp.int32))
    return removed


def on_device(adj_diag, adj_right, alive_diag, alive_right, truss_k):
    within = within_tile(adj_diag & alive_diag)
    across_words = adj_right & alive_right
    across = across_tile(across_words)
    thresh = (truss_k[0] - 2).astype(jnp.float32)
    counts = []
    for step in range(ITERS):
        prev_across = across_tile(shifted(pack_across(across), ROWS, 1))
        next_within = unfold_within(shifted(fold_within(within), ROWS, -1))
        inside, between, new_within, new_across = peel(
            prev_across, within, across, next_within, thresh
        )
        counts.append(tally(within, new_within, across, new_across))
        within, across = (new_within, new_across)
    stacked = jnp.stack(counts)
    stacked = over_axes(stacked, ROWS)
    support = jnp.concatenate(
        [inside * within.astype(jnp.float32), between * across.astype(jnp.float32)], axis=1
    )
    return (support, stacked)


def solution(mesh):
    split = Mesh(mesh.devices.reshape(8, 8, 4, 2), ("rows_0", "rows_1", "rows_2", "rows_3"))
    placed = (P(ROWS, None), P(ROWS, None), P(ROWS, None), P(ROWS, None), P())
    return jax.shard_map(
        on_device, mesh=split, in_specs=placed, out_specs=(P(ROWS, None), P()), check_vma=False
    )
```

profile of v0, /device:TPU:1, one launch (start us, length us, event | category | flops | bytes accessed | tf_op | source)
XLA Modules:
  0.0 128.3 jit_solution(3447967203919431901)
XLA Ops:
  0.7 0.8 and.74
  1.5 0.2 fusion.17
  1.7 0.3 copy.7
  2.1 0.3 fusion.14
  2.4 0.9 rev.18
  3.5 8.7 %collective-permute-start.1 = (s32[8,512]{1,0:T(8,128)S(1)}, s32[8,512]{1,0:T(8,128)S(1)}, u32[]{:S(2)}, u32[]{:S(2)}) collective-permute-start(s32[8,512]{1,0:T(8,128)S(1)} %fusion.25), channel_id=1, source_target_pairs={{0,511},{1,0},{2,1},{3,2},{4,3},{5,4},{6,5},{7,6},{8,7},{9,8},{10,... | collective-permute-start | bytes 49160 | tf_op jit(solution)/shard_map/ppermute | solution.py:13
  12.2 0.4 and_convert_fusion.3
  12.6 1.9 %collective-permute-start = (s32[16,512]{1,0:T(8,128)S(1)}, s32[16,512]{1,0:T(8,128)S(1)}, u32[]{:S(2)}, u32[]{:S(2)}) collective-permute-start(s32[16,512]{1,0:T(8,128)S(1)} %get-tuple-element.9), channel_id=1, source_target_pairs={{0,1},{1,2},{2,3},{3,4},{4,5},{5,6},{6,7},{7,8},{8,9},{9,10},{10,1... | collective-permute-start | bytes 98312 | tf_op jit(solution)/shard_map/ppermute | solution.py:13
  14.6 1.4 %fusion.47 = f32[512,512]{1,0:T(8,128)} fusion(bf16[512,512]{1,0:T(8,128)(2,1)S(1)} %get-tuple-element.17, bf16[512,512]{1,0:T(8,128)(2,1)S(1)} %get-tuple-element.16), kind=kOutput, calls=%fused_computation.93 | convolution fusion | flops 268435456 | bytes 2097152 | tf_op jit(solution)/shard_map/dot_general | solution.py:80
  16.9 0.8 rev.19
  17.6 1.1 pad_add_fusion
  18.7 2.6 %copy.8 = s32[512,512]{0,1:T(8,128)} copy(s32[512,512]{1,0:T(8,128)} %pad_add_fusion) | data formatting | bytes 2097152 | tf_op jit(solution)/shard_map/concatenate | solution.py:65
  21.3 2.2 %fusion.8 = (s32[16,512]{1,0:T(8,128)S(1)}, bf16[512,512]{1,0:T(8,128)(2,1)S(1)}) fusion(bf16[512,512]{1,0:T(8,128)(2,1)S(1)} %get-tuple-element.16, f32[]{:T(128)} %bitcast.4, f32[512,512]{1,0:T(8,128)} %fusion.47, s32[512,512]{0,1:T(8,128)} %copy.8, s32[256,512]{1,0:T(8,128)S(1)} %rev.19, s32[256,512]{1,0:T(8,128)S(1)} %get-tuple-element.14), kind=kOutput, calls=%fused_computation.25 | convolution fusion | flops 270786560 | bytes 4227076 | tf_op jit(solution)/shard_map/dot_general | solution.py:81
  23.5 1.9 %collective-permute-start.4 = (s32[16,512]{1,0:T(8,128)S(1)}, s32[16,512]{1,0:T(8,128)S(1)}, u32[]{:S(2)}, u32[]{:S(2)}) collective-permute-start(s32[16,512]{1,0:T(8,128)S(1)} %get-tuple-element.20), channel_id=1, source_target_pairs={{0,1},{1,2},{2,3},{3,4},{4,5},{5,6},{6,7},{7,8},{8,9},{9,10},{10,1... | collective-permute-start | bytes 98312 | tf_op jit(solution)/shard_map/ppermute | solution.py:13
  25.5 0.5 convolution_bitcast_fusion.2
  26.0 0.4 convolution_add_fusion.8
  26.4 0.5 fusion.7
  26.9 0.9 rev.20
  28.0 10.1 %collective-permute-start.2 = (s32[8,512]{1,0:T(8,128)S(1)}, s32[8,512]{1,0:T(8,128)S(1)}, u32[]{:S(2)}, u32[]{:S(2)}) collective-permute-start(s32[8,512]{1,0:T(8,128)S(1)} %fusion.24), channel_id=1, source_target_pairs={{0,511},{1,0},{2,1},{3,2},{4,3},{5,4},{6,5},{7,6},{8,7},{9,8},{10,... | collective-permute-start | bytes 49160 | tf_op jit(solution)/shard_map/ppermute | solution.py:13
  38.1 0.5 convolution_bitcast_fusion
  38.6 0.4 convolution_add_fusion.4
  39.1 0.5 fusion.6
  39.6 0.9 rev.22
  40.6 9.1 %collective-permute-start.5 = (s32[8,512]{1,0:T(8,128)S(1)}, s32[8,512]{1,0:T(8,128)S(1)}, u32[]{:S(2)}, u32[]{:S(2)}) collective-permute-start(s32[8,512]{1,0:T(8,128)S(1)} %fusion.23), channel_id=1, source_target_pairs={{0,511},{1,0},{2,1},{3,2},{4,3},{5,4},{6,5},{7,6},{8,7},{9,8},{10,... | collective-permute-start | bytes 49160 | tf_op jit(solution)/shard_map/ppermute | solution.py:13
  49.7 1.4 %fusion.48 = f32[512,512]{1,0:T(8,128)} fusion(bf16[512,512]{1,0:T(8,128)(2,1)S(1)} %fusion.7, bf16[512,512]{1,0:T(8,128)(2,1)S(1)} %get-tuple-element.21), kind=kOutput, calls=%fused_computation.94 | convolution fusion | flops 268435456 | bytes 2097152 | tf_op jit(solution)/shard_map/dot_general | solution.py:80
  51.1 1.4 %fusion.28 = (s32[256,512]{1,0:T(8,128)}, s32[256,512]{1,0:T(8,128)}, s32[256,512]{1,0:T(8,128)}, s32[256,512]{1,0:T(8,128)S(1)}) fusion(s32[8,512]{1,0:T(8,128)S(1)} %collective-permute-done.5, s32[256]{0:T(256)S(1)} %shift_left.64, s32[8,512]{1,0:T(8,128)S(1)} %collective-permute-done.2), kind=kLoop, calls=%fused_computation.69 | loop fusion | flops 1310720 | bytes 2130944 | tf_op jit(solution)/shard_map/jit(_where)/select_n | solution.py:63
  52.5 3.9 %rev.21 = s32[256,512]{1,0:T(8,128)S(1)} reverse(s32[256,512]{1,0:T(8,128)} %get-tuple-element.18), dimensions={0,1} | reverse | bytes 1048576 | tf_op jit(solution)/shard_map/rev | solution.py:64
  56.4 1.1 pad_add_fusion.1
  57.5 2.6 %copy.9 = s32[512,512]{0,1:T(8,128)} copy(s32[512,512]{1,0:T(8,128)} %pad_add_fusion.1) | data formatting | bytes 2097152 | tf_op jit(solution)/shard_map/concatenate | solution.py:65
  60.1 2.4 %fusion.9 = (s32[16,512]{1,0:T(8,128)S(1)}, bf16[512,512]{1,0:T(8,128)(2,1)S(1)}) fusion(bf16[512,512]{1,0:T(8,128)(2,1)S(1)} %get-tuple-element.21, f32[]{:T(128)} %bitcast.4, f32[512,512]{1,0:T(8,128)} %fusion.48, s32[512,512]{0,1:T(8,128)} %copy.9, s32[256,512]{1,0:T(8,128)S(1)} %rev.21, s32[256,512]{1,0:T(8,128)} %copy-done.1), kind=kOutput, calls=%fused_computation.27 | convolution fusion | flops 270786560 | bytes 4227076 | tf_op jit(solution)/shard_map/dot_general | solution.py:81
  62.5 1.9 %collective-permute-start.3 = (s32[16,512]{1,0:T(8,128)S(1)}, s32[16,512]{1,0:T(8,128)S(1)}, u32[]{:S(2)}, u32[]{:S(2)}) collective-permute-start(s32[16,512]{1,0:T(8,128)S(1)} %get-tuple-element.24), channel_id=1, source_target_pairs={{0,1},{1,2},{2,3},{3,4},{4,5},{5,6},{6,7},{7,8},{8,9},{9,10},{10,1... | collective-permute-start | bytes 98312 | tf_op jit(solution)/shard_map/ppermute | solution.py:13
  64.4 3.8 %rev.23 = s32[256,512]{1,0:T(8,128)S(1)} reverse(s32[256,512]{1,0:T(8,128)} %get-tuple-element.11), dimensions={0,1} | reverse | bytes 1048576 | tf_op jit(solution)/shard_map/rev | solution.py:64
  68.2 2.1 %pad_add_fusion.2 = s32[512,512]{1,0:T(8,128)} fusion(s32[256,512]{1,0:T(8,128)S(1)} %rev.23, s32[256,512]{1,0:T(8,128)} %get-tuple-element.10), kind=kLoop, calls=%fused_computation.23 | loop fusion | flops 262144 | bytes 2097152 | tf_op jit(solution)/shard_map/concatenate | solution.py:65
  70.3 2.5 %copy.13 = s32[512,512]{0,1:T(8,128)} copy(s32[512,512]{1,0:T(8,128)} %pad_add_fusion.2) | data formatting | bytes 2097152 | tf_op jit(solution)/shard_map/concatenate | solution.py:65
  72.8 0.4 fusion.49
  73.3 0.6 copy-done
  73.9 0.3 copy-done.3
  74.2 1.5 %convert_multiply_fusion = (f32[512,512]{1,0:T(8,128)}, f32[512,512]{1,0:T(8,128)S(1)}) fusion(bf16[512,512]{1,0:T(8,128)(2,1)S(1)} %get-tuple-element.25, f32[]{:T(128)} %bitcast.4, f32[512,512]{1,0:T(8,128)S(1)} %fusion.49, s32[512,512]{0,1:T(8,128)S(1)} %copy-done.3, s32[256,512]{1,0:T(8,128)S(1)} %rev.23, s32[256,512]{1,0:T(8,128)S(1)} %copy-done), kind=kOutput, calls=%fused_computation.48 | convolution fusion | flops 270532608 | bytes 5767172 | tf_op jit(solution)/shard_map/dot_general | solution.py:81
  75.7 1.5 %convert_reduce_fusion.4 = (s32[]{:T(128)}, s32[]{:T(128)}, s32[]{:T(128)}) fusion(bf16[512,512]{1,0:T(8,128)(2,1)S(1)} %get-tuple-element.21, s32[512]{0:T(512)S(1)} %shift_right_arithmetic.162, s32[16,512]{1,0:T(8,128)S(1)} %and.71, bf16[512,512]{1,0:T(8,128)(2,1)S(1)} %get-tuple-element.25, f32[512,512]{1,0:T(8,128)S(1)} %get-tuple-element.23, f32[]{:T(128)} %bitcast.4), kind=kLoop, calls=%fused_computation.46 | loop fusion | flops 4718589 | bytes 2131984 | tf_op jit(solution)/shard_map/reduce_sum | solution.py:101
  77.2 0.5 convolution_bitcast_fusion.1
  77.7 0.4 convolution_add_fusion.2
  78.1 1.5 %convert_multiply_fusion.1 = (f32[512,512]{1,0:T(8,128)}, f32[512,512]{1,0:T(8,128)S(1)}) fusion(bf16[512,512]{1,0:T(8,128)(2,1)S(1)} %fusion.6, f32[]{:T(128)} %bitcast.4, f32[512,512]{1,0:T(8,128)S(1)} %convolution_add_fusion.2, bf16[512,512]{1,0:T(8,128)(2,1)S(1)} %get-tuple-element.25), kind=kOutput, calls=%fused_computation.49 | convolution fusion | flops 269746176 | bytes 4194308 | tf_op jit(solution)/shard_map/dot_general | solution.py:74
  79.6 1.4 %convert_reduce_fusion.5 = (s32[]{:T(128)}, s32[]{:T(128)}, s32[]{:T(128)}) fusion(bf16[512,512]{1,0:T(8,128)(2,1)S(1)} %get-tuple-element.17, bf16[512,512]{1,0:T(8,128)(2,1)S(1)} %fusion.7, bf16[512,512]{1,0:T(8,128)(2,1)S(1)} %fusion.6, f32[512,512]{1,0:T(8,128)S(1)} %get-tuple-element.27, f32[]{:T(128)} %bitcast.4), kind=kLoop, calls=%fused_computation.47 | loop fusion | flops 2883581 | bytes 2621456 | tf_op jit(solution)/shard_map/reduce_sum | solution.py:100
  90.5 7.0 %psum.28 = s32[3]{0:T(128)S(1)} all-reduce(s32[3]{0:T(128)S(1)} %pad_add_fusion.3), channel_id=1, replica_groups=mesh['rows_0'=8,'rows_1'=8,'rows_2'=4,'rows_3'=2] {'rows_0'}, use_global_device_ids=true, to_apply=%region_12.13 | all-reduce | flops 3 | bytes 24 | tf_op jit(solution)/shard_map/psum | solution.py:18
  97.5 7.0 %psum.29 = s32[3]{0:T(128)S(1)} all-reduce(s32[3]{0:T(128)S(1)} %psum.28), channel_id=1, replica_groups=mesh['rows_0'=8,'rows_1'=8,'rows_2'=4,'rows_3'=2] {'rows_1'}, use_global_device_ids=true, to_apply=%region_13.14 | all-reduce | flops 3 | bytes 24 | tf_op jit(solution)/shard_map/psum | solution.py:18
  104.5 11.6 %psum.30 = s32[3]{0:T(128)S(1)} all-reduce(s32[3]{0:T(128)S(1)} %psum.29), channel_id=1, replica_groups=mesh['rows_0'=8,'rows_1'=8,'rows_2'=4,'rows_3'=2] {'rows_2'}, use_global_device_ids=true, to_apply=%region_14.15 | all-reduce | flops 3 | bytes 24 | tf_op jit(solution)/shard_map/psum | solution.py:18
  116.1 9.4 %psum.31 = s32[3]{0:T(128)} all-reduce(s32[3]{0:T(128)S(1)} %psum.30), channel_id=1, replica_groups=mesh['rows_0'=8,'rows_1'=8,'rows_2'=4,'rows_3'=2] {'rows_3'}, use_global_device_ids=true, to_apply=%region_15.16 | all-reduce | flops 3 | bytes 24 | tf_op jit(solution)/shard_map/psum | solution.py:18
  125.5 2.8 %pad_maximum_fusion = f32[512,1024]{1,0:T(8,128)} fusion(f32[512,512]{1,0:T(8,128)} %get-tuple-element.22, f32[512,512]{1,0:T(8,128)S(1)} %copy-done.2), kind=kLoop, calls=%fused_computation | loop fusion | flops 524288 | bytes 4194304 | tf_op jit(solution)/shard_map/concatenate | solution.py:121
  (29 shorter events, 0.9 us)
Async XLA Ops:
  0.6 1.4 %copy-start.4 = (s32[16,512]{1,0:T(8,128)S(1)}, s32[16,512]{1,0:T(8,128)}, u32[]{:S(2)}) copy-start(s32[16,512]{1,0:T(8,128)} %param.6) | copy-start | bytes 98308
  0.6 1.4 %copy-start.5 = (s32[16,512]{1,0:T(8,128)S(1)}, s32[16,512]{1,0:T(8,128)}, u32[]{:S(2)}) copy-start(s32[16,512]{1,0:T(8,128)} %param.8) | copy-start | bytes 98308
  3.5 13.2 %collective-permute-start.1 = (s32[8,512]{1,0:T(8,128)S(1)}, s32[8,512]{1,0:T(8,128)S(1)}, u32[]{:S(2)}, u32[]{:S(2)}) collective-permute-start(s32[8,512]{1,0:T(8,128)S(1)} %fusion.25), channel_id=1, source_target_pairs={{0,511},{1,0},{2,1},{3,2},{4,3},{5,4},{6,5},{7,6},{8,7},{9,8},{10,... | collective-permute-start | bytes 49160 | tf_op jit(solution)/shard_map/ppermute | solution.py:13
  12.6 12.8 %collective-permute-start = (s32[16,512]{1,0:T(8,128)S(1)}, s32[16,512]{1,0:T(8,128)S(1)}, u32[]{:S(2)}, u32[]{:S(2)}) collective-permute-start(s32[16,512]{1,0:T(8,128)S(1)} %get-tuple-element.9), channel_id=1, source_target_pairs={{0,1},{1,2},{2,3},{3,4},{4,5},{5,6},{6,7},{7,8},{8,9},{9,10},{10,1... | collective-permute-start | bytes 98312 | tf_op jit(solution)/shard_map/ppermute | solution.py:13
  23.5 14.6 %collective-permute-start.4 = (s32[16,512]{1,0:T(8,128)S(1)}, s32[16,512]{1,0:T(8,128)S(1)}, u32[]{:S(2)}, u32[]{:S(2)}) collective-permute-start(s32[16,512]{1,0:T(8,128)S(1)} %get-tuple-element.20), channel_id=1, source_target_pairs={{0,1},{1,2},{2,3},{3,4},{4,5},{5,6},{6,7},{7,8},{8,9},{9,10},{10,1... | collective-permute-start | bytes 98312 | tf_op jit(solution)/shard_map/ppermute | solution.py:13
  28.0 23.1 %collective-permute-start.2 = (s32[8,512]{1,0:T(8,128)S(1)}, s32[8,512]{1,0:T(8,128)S(1)}, u32[]{:S(2)}, u32[]{:S(2)}) collective-permute-start(s32[8,512]{1,0:T(8,128)S(1)} %fusion.24), channel_id=1, source_target_pairs={{0,511},{1,0},{2,1},{3,2},{4,3},{5,4},{6,5},{7,6},{8,7},{9,8},{10,... | collective-permute-start | bytes 49160 | tf_op jit(solution)/shard_map/ppermute | solution.py:13
  40.6 10.5 %collective-permute-start.5 = (s32[8,512]{1,0:T(8,128)S(1)}, s32[8,512]{1,0:T(8,128)S(1)}, u32[]{:S(2)}, u32[]{:S(2)}) collective-permute-start(s32[8,512]{1,0:T(8,128)S(1)} %fusion.23), channel_id=1, source_target_pairs={{0,511},{1,0},{2,1},{3,2},{4,3},{5,4},{6,5},{7,6},{8,7},{9,8},{10,... | collective-permute-start | bytes 49160 | tf_op jit(solution)/shard_map/ppermute | solution.py:13
  52.5 5.0 %copy-start.1 = (s32[256,512]{1,0:T(8,128)}, s32[256,512]{1,0:T(8,128)S(1)}, u32[]{:S(2)}) copy-start(s32[256,512]{1,0:T(8,128)S(1)} %get-tuple-element.19) | copy-start | bytes 1572868
  62.5 14.7 %collective-permute-start.3 = (s32[16,512]{1,0:T(8,128)S(1)}, s32[16,512]{1,0:T(8,128)S(1)}, u32[]{:S(2)}, u32[]{:S(2)}) collective-permute-start(s32[16,512]{1,0:T(8,128)S(1)} %get-tuple-element.24), channel_id=1, source_target_pairs={{0,1},{1,2},{2,3},{3,4},{4,5},{5,6},{6,7},{7,8},{8,9},{9,10},{10,1... | collective-permute-start | bytes 98312 | tf_op jit(solution)/shard_map/ppermute | solution.py:13
  72.8 1.0 copy-start
  72.8 1.4 %copy-start.3 = (s32[512,512]{0,1:T(8,128)S(1)}, s32[512,512]{0,1:T(8,128)}, u32[]{:S(2)}) copy-start(s32[512,512]{0,1:T(8,128)} %copy.13) | copy-start | bytes 3145732
  79.6 45.9 %copy-start.2 = (f32[512,512]{1,0:T(8,128)S(1)}, f32[512,512]{1,0:T(8,128)}, u32[]{:S(2)}) copy-start(f32[512,512]{1,0:T(8,128)} %get-tuple-element.26) | copy-start | bytes 3145732
where the time goes:
time: 129 us; the launch traced here: 128 us
  blocking collectives  35 us (27%)
  starting transfers between devices  33.7 us (26%)
  local copies, waits for them, and re-layouts  20.4 us (16%)
  matrix products  14.6 us (11%)
  other arithmetic  13.6 us (11%)
  between operations  11.1 us (9%)
    psum x4, blocking collectives, over_axes(): array = lax.psum(array, axis)  35 us
    ppermute x6, starting transfers between devices, shifted(): lax.ppermute(array, axis, [(i, (i + by) % count) for i in range(count)])  33.7 us
    rev x3, local copies, waits for them, and re-layouts, unfold_within(): jnp.where(col_ids < row_ids, folded, jnp.zeros_like(folded))[::-1, ::-1]  8.42 us
    concatenate x3, local copies, waits for them, and re-layouts, unfold_within(): upper_half = jnp.concatenate([top_rows, bottom_rows], axis=0)  7.69 us
    dot_general x3, matrix products, support_across(): jnp.dot(across, next_within, preferred_element_type=jnp.float32)  6.13 us
    concatenate x3, other arithmetic, unfold_within(): upper_half = jnp.concatenate([top_rows, bottom_rows], axis=0)  4.27 us
    dot_general x3, matrix products, support_across(): between = jnp.dot(within, across, preferred_element_type=jnp.float32)  3.25 us
    concatenate x1, other arithmetic, on_device(): jnp.concatenate([inside * within.astype(jnp.float32), between * across.as...  2.76 us
  transfers between devices with their start and end apart: 6, of which 0 were waited for; matrix products, arithmetic and copies ran while one was open for 21% of the time, Pallas kernels for 0%

commit v1 on v0

--- a/solution.py
+++ b/solution.py
@@ -15,7 +15,7 @@
 
 def over_axes(array, axes):
     for axis in axes:
-        array = lax.psum(array, axis)
+        array = jnp.sum(lax.all_gather(array, axis), axis=0)
     return array
 
 

time: 129 us -> 139 us (1.078)
  local copies, waits for them, and re-layouts: 20.4 us -> 26.6 us
  between operations: 11.1 us -> 13.6 us
    psum x4 -> x0, blocking collectives: 35 us -> none  [over_axes(): array = lax.psum(array, axis)]
    unnamed x0 -> x4, blocking collectives: none -> 34.5 us
    unnamed x12 -> x23, local copies, waits for them, and re-layouts: 0.97 us -> 6.92 us
  transfers between devices with their start and end apart: 6 -> 6, of which waited for: 0 -> 0; matrix products, arithmetic and copies ran while one was open for 21% -> 23% of each run, Pallas kernels for 0% -> 0%
where the time goes in v1:
time: 139 us; the launch traced here: 137 us
  blocking collectives  34.5 us (25%)
  starting transfers between devices  33.7 us (24%)
  local copies, waits for them, and re-layouts  26.6 us (19%)
  matrix products  14.6 us (11%)
  other arithmetic  14.3 us (10%)
  between operations  13.6 us (10%)
    unnamed x4, blocking collectives  34.5 us
    ppermute x6, starting transfers between devices, shifted(): lax.ppermute(array, axis, [(i, (i + by) % count) for i in range(count)])  33.7 us
    rev x3, local copies, waits for them, and re-layouts, unfold_within(): jnp.where(col_ids < row_ids, folded, jnp.zeros_like(folded))[::-1, ::-1]  8.42 us
    concatenate x3, local copies, waits for them, and re-layouts, unfold_within(): upper_half = jnp.concatenate([top_rows, bottom_rows], axis=0)  7.69 us
    unnamed x23, local copies, waits for them, and re-layouts  6.92 us
    dot_general x3, matrix products, support_across(): jnp.dot(across, next_within, preferred_element_type=jnp.float32)  6.13 us
    concatenate x3, other arithmetic, unfold_within(): upper_half = jnp.concatenate([top_rows, bottom_rows], axis=0)  4.27 us
    dot_general x3, matrix products, support_across(): between = jnp.dot(within, across, preferred_element_type=jnp.float32)  3.25 us
  transfers between devices with their start and end apart: 6, of which 0 were waited for; matrix products, arithmetic and copies ran while one was open for 23% of the time, Pallas kernels for 0%

profile of v1, /device:TPU:1, one launch (start us, length us, event | category | flops | bytes accessed | tf_op | source)
XLA Modules:
  0.0 137.3 jit_solution(16279163036087495224)
XLA Ops:
  0.7 0.8 and.74
  2.4 0.9 rev.18
  3.5 8.7 %collective-permute-start.1 = (s32[8,512]{1,0:T(8,128)S(1)}, s32[8,512]{1,0:T(8,128)S(1)}, u32[]{:S(2)}, u32[]{:S(2)}) collective-permute-start(s32[8,512]{1,0:T(8,128)S(1)} %fusion.25), channel_id=1, source_target_pairs={{0,511},{1,0},{2,1},{3,2},{4,3},{5,4},{6,5},{7,6},{8,7},{9,8},{10,... | collective-permute-start | bytes 49160 | tf_op jit(solution)/shard_map/ppermute | solution.py:13
  12.6 1.9 %collective-permute-start = (s32[16,512]{1,0:T(8,128)S(1)}, s32[16,512]{1,0:T(8,128)S(1)}, u32[]{:S(2)}, u32[]{:S(2)}) collective-permute-start(s32[16,512]{1,0:T(8,128)S(1)} %get-tuple-element.9), channel_id=1, source_target_pairs={{0,1},{1,2},{2,3},{3,4},{4,5},{5,6},{6,7},{7,8},{8,9},{9,10},{10,1... | collective-permute-start | bytes 98312 | tf_op jit(solution)/shard_map/ppermute | solution.py:13
  14.6 1.4 %fusion.47 = f32[512,512]{1,0:T(8,128)} fusion(bf16[512,512]{1,0:T(8,128)(2,1)S(1)} %get-tuple-element.17, bf16[512,512]{1,0:T(8,128)(2,1)S(1)} %get-tuple-element.16), kind=kOutput, calls=%fused_computation.93 | convolution fusion | flops 268435456 | bytes 2097152 | tf_op jit(solution)/shard_map/dot_general | solution.py:80
  16.7 1.3 dynamic-slice
  18.1 1.3 dynamic-slice.1
  20.7 1.3 dynamic-slice.2
  22.6 1.3 dynamic-slice.3
  24.0 0.8 rev.19
  24.8 1.1 pad_add_fusion
  25.9 2.6 %copy.17 = s32[512,512]{0,1:T(8,128)} copy(s32[512,512]{1,0:T(8,128)} %pad_add_fusion) | data formatting | bytes 2097152 | tf_op jit(solution)/shard_map/concatenate | solution.py:65
  28.5 2.2 %fusion.8 = (s32[16,512]{1,0:T(8,128)S(1)}, bf16[512,512]{1,0:T(8,128)(2,1)S(1)}) fusion(bf16[512,512]{1,0:T(8,128)(2,1)S(1)} %get-tuple-element.16, f32[]{:T(128)} %bitcast.4, f32[512,512]{1,0:T(8,128)} %fusion.47, s32[512,512]{0,1:T(8,128)} %copy.17, s32[256,512]{1,0:T(8,128)S(1)} %rev.19, s32[256,512]{1,0:T(8,128)S(1)} %get-tuple-element.14), kind=kOutput, calls=%fused_computation.25 | convolution fusion | flops 270786560 | bytes 4227076 | tf_op jit(solution)/shard_map/dot_general | solution.py:81
  30.7 1.9 %collective-permute-start.4 = (s32[16,512]{1,0:T(8,128)S(1)}, s32[16,512]{1,0:T(8,128)S(1)}, u32[]{:S(2)}, u32[]{:S(2)}) collective-permute-start(s32[16,512]{1,0:T(8,128)S(1)} %get-tuple-element.20), channel_id=1, source_target_pairs={{0,1},{1,2},{2,3},{3,4},{4,5},{5,6},{6,7},{7,8},{8,9},{9,10},{10,1... | collective-permute-start | bytes 98312 | tf_op jit(solution)/shard_map/ppermute | solution.py:13
  32.6 0.5 convolution_bitcast_fusion.2
  33.1 0.4 convolution_add_fusion.8
  33.6 0.5 fusion.7
  34.1 0.9 rev.20
  35.2 10.1 %collective-permute-start.2 = (s32[8,512]{1,0:T(8,128)S(1)}, s32[8,512]{1,0:T(8,128)S(1)}, u32[]{:S(2)}, u32[]{:S(2)}) collective-permute-start(s32[8,512]{1,0:T(8,128)S(1)} %fusion.24), channel_id=1, source_target_pairs={{0,511},{1,0},{2,1},{3,2},{4,3},{5,4},{6,5},{7,6},{8,7},{9,8},{10,... | collective-permute-start | bytes 49160 | tf_op jit(solution)/shard_map/ppermute | solution.py:13
  45.3 0.5 convolution_bitcast_fusion
  45.8 0.4 convolution_add_fusion.4
  46.2 0.5 fusion.6
  46.8 0.9 rev.22
  47.8 9.1 %collective-permute-start.5 = (s32[8,512]{1,0:T(8,128)S(1)}, s32[8,512]{1,0:T(8,128)S(1)}, u32[]{:S(2)}, u32[]{:S(2)}) collective-permute-start(s32[8,512]{1,0:T(8,128)S(1)} %fusion.23), channel_id=1, source_target_pairs={{0,511},{1,0},{2,1},{3,2},{4,3},{5,4},{6,5},{7,6},{8,7},{9,8},{10,... | collective-permute-start | bytes 49160 | tf_op jit(solution)/shard_map/ppermute | solution.py:13
  56.9 1.4 %fusion.48 = f32[512,512]{1,0:T(8,128)} fusion(bf16[512,512]{1,0:T(8,128)(2,1)S(1)} %fusion.7, bf16[512,512]{1,0:T(8,128)(2,1)S(1)} %get-tuple-element.21), kind=kOutput, calls=%fused_computation.94 | convolution fusion | flops 268435456 | bytes 2097152 | tf_op jit(solution)/shard_map/dot_general | solution.py:80
  58.3 1.4 %fusion.28 = (s32[256,512]{1,0:T(8,128)}, s32[256,512]{1,0:T(8,128)}, s32[256,512]{1,0:T(8,128)}, s32[256,512]{1,0:T(8,128)S(1)}) fusion(s32[8,512]{1,0:T(8,128)S(1)} %collective-permute-done.5, s32[256]{0:T(256)S(1)} %shift_left.64, s32[8,512]{1,0:T(8,128)S(1)} %collective-permute-done.2), kind=kLoop, calls=%fused_computation.69 | loop fusion | flops 1310720 | bytes 2130944 | tf_op jit(solution)/shard_map/jit(_where)/select_n | solution.py:63
  59.7 3.9 %rev.21 = s32[256,512]{1,0:T(8,128)S(1)} reverse(s32[256,512]{1,0:T(8,128)} %get-tuple-element.18), dimensions={0,1} | reverse | bytes 1048576 | tf_op jit(solution)/shard_map/rev | solution.py:64
  63.6 1.1 pad_add_fusion.1
  64.7 2.6 %copy.18 = s32[512,512]{0,1:T(8,128)} copy(s32[512,512]{1,0:T(8,128)} %pad_add_fusion.1) | data formatting | bytes 2097152 | tf_op jit(solution)/shard_map/concatenate | solution.py:65
  67.3 2.4 %fusion.9 = (s32[16,512]{1,0:T(8,128)S(1)}, bf16[512,512]{1,0:T(8,128)(2,1)S(1)}) fusion(bf16[512,512]{1,0:T(8,128)(2,1)S(1)} %get-tuple-element.21, f32[]{:T(128)} %bitcast.4, f32[512,512]{1,0:T(8,128)} %fusion.48, s32[512,512]{0,1:T(8,128)} %copy.18, s32[256,512]{1,0:T(8,128)S(1)} %rev.21, s32[256,512]{1,0:T(8,128)} %copy-done.1), kind=kOutput, calls=%fused_computation.27 | convolution fusion | flops 270786560 | bytes 4227076 | tf_op jit(solution)/shard_map/dot_general | solution.py:81
  69.7 1.9 %collective-permute-start.3 = (s32[16,512]{1,0:T(8,128)S(1)}, s32[16,512]{1,0:T(8,128)S(1)}, u32[]{:S(2)}, u32[]{:S(2)}) collective-permute-start(s32[16,512]{1,0:T(8,128)S(1)} %get-tuple-element.24), channel_id=1, source_target_pairs={{0,1},{1,2},{2,3},{3,4},{4,5},{5,6},{6,7},{7,8},{8,9},{9,10},{10,1... | collective-permute-start | bytes 98312 | tf_op jit(solution)/shard_map/ppermute | solution.py:13
  71.6 3.8 %rev.23 = s32[256,512]{1,0:T(8,128)S(1)} reverse(s32[256,512]{1,0:T(8,128)} %get-tuple-element.11), dimensions={0,1} | reverse | bytes 1048576 | tf_op jit(solution)/shard_map/rev | solution.py:64
  75.4 2.1 %pad_add_fusion.2 = s32[512,512]{1,0:T(8,128)} fusion(s32[256,512]{1,0:T(8,128)S(1)} %rev.23, s32[256,512]{1,0:T(8,128)} %get-tuple-element.10), kind=kLoop, calls=%fused_computation.23 | loop fusion | flops 262144 | bytes 2097152 | tf_op jit(solution)/shard_map/concatenate | solution.py:65
  77.5 2.5 %copy.22 = s32[512,512]{0,1:T(8,128)} copy(s32[512,512]{1,0:T(8,128)} %pad_add_fusion.2) | data formatting | bytes 2097152 | tf_op jit(solution)/shard_map/concatenate | solution.py:65
  80.0 0.4 fusion.49
  80.5 0.6 copy-done
  81.4 1.5 %convert_multiply_fusion = (f32[512,512]{1,0:T(8,128)}, f32[512,512]{1,0:T(8,128)S(1)}) fusion(bf16[512,512]{1,0:T(8,128)(2,1)S(1)} %get-tuple-element.25, f32[]{:T(128)} %bitcast.4, f32[512,512]{1,0:T(8,128)S(1)} %fusion.49, s32[512,512]{0,1:T(8,128)S(1)} %copy-done.3, s32[256,512]{1,0:T(8,128)S(1)} %rev.23, s32[256,512]{1,0:T(8,128)S(1)} %copy-done), kind=kOutput, calls=%fused_computation.48 | convolution fusion | flops 270532608 | bytes 5767172 | tf_op jit(solution)/shard_map/dot_general | solution.py:81
  82.9 1.5 %convert_reduce_fusion.4 = (s32[]{:T(128)}, s32[]{:T(128)}, s32[]{:T(128)}) fusion(bf16[512,512]{1,0:T(8,128)(2,1)S(1)} %get-tuple-element.21, s32[512]{0:T(512)S(1)} %shift_right_arithmetic.162, s32[16,512]{1,0:T(8,128)S(1)} %and.71, bf16[512,512]{1,0:T(8,128)(2,1)S(1)} %get-tuple-element.25, f32[512,512]{1,0:T(8,128)S(1)} %get-tuple-element.23, f32[]{:T(128)} %bitcast.4), kind=kLoop, calls=%fused_computation.46 | loop fusion | flops 4718589 | bytes 2131984 | tf_op jit(solution)/shard_map/reduce_sum | solution.py:101
  84.4 0.5 convolution_bitcast_fusion.1
  84.9 0.4 convolution_add_fusion.2
  85.3 1.5 %convert_multiply_fusion.1 = (f32[512,512]{1,0:T(8,128)}, f32[512,512]{1,0:T(8,128)S(1)}) fusion(bf16[512,512]{1,0:T(8,128)(2,1)S(1)} %fusion.6, f32[]{:T(128)} %bitcast.4, f32[512,512]{1,0:T(8,128)S(1)} %convolution_add_fusion.2, bf16[512,512]{1,0:T(8,128)(2,1)S(1)} %get-tuple-element.25), kind=kOutput, calls=%fused_computation.49 | convolution fusion | flops 269746176 | bytes 4194308 | tf_op jit(solution)/shard_map/dot_general | solution.py:74
  86.8 1.4 %convert_reduce_fusion.5 = (s32[]{:T(128)}, s32[]{:T(128)}, s32[]{:T(128)}) fusion(bf16[512,512]{1,0:T(8,128)(2,1)S(1)} %get-tuple-element.17, bf16[512,512]{1,0:T(8,128)(2,1)S(1)} %fusion.7, bf16[512,512]{1,0:T(8,128)(2,1)S(1)} %fusion.6, f32[512,512]{1,0:T(8,128)S(1)} %get-tuple-element.27, f32[]{:T(128)} %bitcast.4), kind=kLoop, calls=%fused_computation.47 | loop fusion | flops 2883581 | bytes 2621456 | tf_op jit(solution)/shard_map/reduce_sum | solution.py:100
  97.8 7.0 %all-reduce = s32[24]{0:T(128)S(1)} all-reduce(s32[24]{0:T(128)S(1)} %add_dynamic-update-slice_fusion), channel_id=2, replica_groups=mesh['rows_0'=8,'rows_1'=8,'rows_2'=4,'rows_3'=2] {'rows_0'}, use_global_device_ids=true, to_apply=%add | all-reduce | flops 24 | bytes 192
  105.2 7.0 %all-reduce.1 = s32[24]{0:T(128)S(1)} all-reduce(s32[24]{0:T(128)S(1)} %dynamic-update-slice.1), channel_id=3, replica_groups=mesh['rows_0'=8,'rows_1'=8,'rows_2'=4,'rows_3'=2] {'rows_1'}, use_global_device_ids=true, to_apply=%add.1 | all-reduce | flops 24 | bytes 192
  113.1 11.6 %all-reduce.2 = s32[12]{0:T(128)S(1)} all-reduce(s32[12]{0:T(128)S(1)} %dynamic-update-slice.2), channel_id=4, replica_groups=mesh['rows_0'=8,'rows_1'=8,'rows_2'=4,'rows_3'=2] {'rows_2'}, use_global_device_ids=true, to_apply=%add.2 | all-reduce | flops 12 | bytes 96
  125.0 8.9 %all-reduce.3 = s32[6]{0:T(128)S(1)} all-reduce(s32[6]{0:T(128)S(1)} %dynamic-update-slice.3), channel_id=5, replica_groups=mesh['rows_0'=8,'rows_1'=8,'rows_2'=4,'rows_3'=2] {'rows_3'}, use_global_device_ids=true, to_apply=%add.3 | all-reduce | flops 6 | bytes 48
  134.0 0.5 reduce_sum.159
  134.6 2.8 %pad_maximum_fusion = f32[512,1024]{1,0:T(8,128)} fusion(f32[512,512]{1,0:T(8,128)} %get-tuple-element.22, f32[512,512]{1,0:T(8,128)S(1)} %copy-done.2), kind=kLoop, calls=%fused_computation | loop fusion | flops 524288 | bytes 4194304 | tf_op jit(solution)/shard_map/concatenate | solution.py:121
  (48 shorter events, 3.7 us)
Async XLA Ops:
  0.6 1.4 %copy-start.4 = (s32[16,512]{1,0:T(8,128)S(1)}, s32[16,512]{1,0:T(8,128)}, u32[]{:S(2)}) copy-start(s32[16,512]{1,0:T(8,128)} %param.6) | copy-start | bytes 98308
  0.6 1.4 %copy-start.5 = (s32[16,512]{1,0:T(8,128)S(1)}, s32[16,512]{1,0:T(8,128)}, u32[]{:S(2)}) copy-start(s32[16,512]{1,0:T(8,128)} %param.8) | copy-start | bytes 98308
  3.5 20.4 %collective-permute-start.1 = (s32[8,512]{1,0:T(8,128)S(1)}, s32[8,512]{1,0:T(8,128)S(1)}, u32[]{:S(2)}, u32[]{:S(2)}) collective-permute-start(s32[8,512]{1,0:T(8,128)S(1)} %fusion.25), channel_id=1, source_target_pairs={{0,511},{1,0},{2,1},{3,2},{4,3},{5,4},{6,5},{7,6},{8,7},{9,8},{10,... | collective-permute-start | bytes 49160 | tf_op jit(solution)/shard_map/ppermute | solution.py:13
  12.6 20.0 %collective-permute-start = (s32[16,512]{1,0:T(8,128)S(1)}, s32[16,512]{1,0:T(8,128)S(1)}, u32[]{:S(2)}, u32[]{:S(2)}) collective-permute-start(s32[16,512]{1,0:T(8,128)S(1)} %get-tuple-element.9), channel_id=1, source_target_pairs={{0,1},{1,2},{2,3},{3,4},{4,5},{5,6},{6,7},{7,8},{8,9},{9,10},{10,1... | collective-permute-start | bytes 98312 | tf_op jit(solution)/shard_map/ppermute | solution.py:13
  30.7 14.6 %collective-permute-start.4 = (s32[16,512]{1,0:T(8,128)S(1)}, s32[16,512]{1,0:T(8,128)S(1)}, u32[]{:S(2)}, u32[]{:S(2)}) collective-permute-start(s32[16,512]{1,0:T(8,128)S(1)} %get-tuple-element.20), channel_id=1, source_target_pairs={{0,1},{1,2},{2,3},{3,4},{4,5},{5,6},{6,7},{7,8},{8,9},{9,10},{10,1... | collective-permute-start | bytes 98312 | tf_op jit(solution)/shard_map/ppermute | solution.py:13
  35.2 23.2 %collective-permute-start.2 = (s32[8,512]{1,0:T(8,128)S(1)}, s32[8,512]{1,0:T(8,128)S(1)}, u32[]{:S(2)}, u32[]{:S(2)}) collective-permute-start(s32[8,512]{1,0:T(8,128)S(1)} %fusion.24), channel_id=1, source_target_pairs={{0,511},{1,0},{2,1},{3,2},{4,3},{5,4},{6,5},{7,6},{8,7},{9,8},{10,... | collective-permute-start | bytes 49160 | tf_op jit(solution)/shard_map/ppermute | solution.py:13
  47.8 10.5 %collective-permute-start.5 = (s32[8,512]{1,0:T(8,128)S(1)}, s32[8,512]{1,0:T(8,128)S(1)}, u32[]{:S(2)}, u32[]{:S(2)}) collective-permute-start(s32[8,512]{1,0:T(8,128)S(1)} %fusion.23), channel_id=1, source_target_pairs={{0,511},{1,0},{2,1},{3,2},{4,3},{5,4},{6,5},{7,6},{8,7},{9,8},{10,... | collective-permute-start | bytes 49160 | tf_op jit(solution)/shard_map/ppermute | solution.py:13
  59.7 5.0 %copy-start.1 = (s32[256,512]{1,0:T(8,128)}, s32[256,512]{1,0:T(8,128)S(1)}, u32[]{:S(2)}) copy-start(s32[256,512]{1,0:T(8,128)S(1)} %get-tuple-element.19) | copy-start | bytes 1572868
  69.7 14.7 %collective-permute-start.3 = (s32[16,512]{1,0:T(8,128)S(1)}, s32[16,512]{1,0:T(8,128)S(1)}, u32[]{:S(2)}, u32[]{:S(2)}) collective-permute-start(s32[16,512]{1,0:T(8,128)S(1)} %get-tuple-element.24), channel_id=1, source_target_pairs={{0,1},{1,2},{2,3},{3,4},{4,5},{5,6},{6,7},{7,8},{8,9},{9,10},{10,1... | collective-permute-start | bytes 98312 | tf_op jit(solution)/shard_map/ppermute | solution.py:13
  80.0 1.0 copy-start
  80.0 1.4 %copy-start.3 = (s32[512,512]{0,1:T(8,128)S(1)}, s32[512,512]{0,1:T(8,128)}, u32[]{:S(2)}) copy-start(s32[512,512]{0,1:T(8,128)} %copy.22) | copy-start | bytes 3145732
  86.8 47.8 %copy-start.2 = (f32[512,512]{1,0:T(8,128)S(1)}, f32[512,512]{1,0:T(8,128)}, u32[]{:S(2)}) copy-start(f32[512,512]{1,0:T(8,128)} %get-tuple-element.26) | copy-start | bytes 3145732
